TPU v7x, 256 devices: a whole 4x4x8 slice. The times are simulated.
256 devices in a mesh: seq: 32 (over z, x), exp: 8 (over y, core).
Axes of the slice: x: 4, y: 4, z: 8, core: 2. Of those that a mesh axis runs over, the one named last changes fastest.
Arguments:
- tokens: bfloat16 [32768, 2560], P(('seq', 'exp')), may hold values from -6 to 6
- routes: int32 [32768, 1], P(('seq', 'exp')), may hold values from 0 to 15; in each aligned block of 128 rows (0 to 127, 128 to 255, ...) at most 16 rows name the same one
- gate_inner_weight: bfloat16 [2560, 2, 3072], P(None, None, 'exp'), may hold values from -0.125 to 0.125
- state_map_weight: bfloat16 [2560, 256], replicated, may hold values from -0.125 to 0.125
- step_size_weight: bfloat16 [2560, 48], P(None, 'exp'), may hold values from -0.125 to 0.125
- adapter_down_weight: bfloat16 [2560, 128], P(None, 'exp'), may hold values from -0.125 to 0.125
- adapter_up_weight: bfloat16 [128, 2, 3072], P(None, None, 'exp'), may hold values from -1.5 to 1.5
- inner_conv_taps: float32 [4, 3072], P(None, 'exp'), may hold values from -3 to 3
- state_map_taps: float32 [4, 256], replicated, may hold values from -3 to 3
- inner_conv_bias: float32 [3072], P('exp'), may hold values from -3 to 3
- state_map_conv_bias: float32 [256], replicated, may hold values from -3 to 3
- step_size_bias: float32 [48], P('exp'), may hold values from -6 to -3
- head_decay_rate: float32 [48], P('exp'), may hold values from 4.656613e-06 to 8
- direct_head_scale: float32 [48], P('exp'), may hold values from 0.5 to 2
- gated_norm_scale: float32 [3072], P('exp'), may hold values from 0.5 to 1.5
Outputs:
- mixed: bfloat16 [32768, 3072], P('seq', 'exp')
Inputs may be any that keep to these rules, and one draw needn't show every extreme that they name: `routes`: among the rows of one device no expert is named more than 16 times.
All inputs are finite; a program needn't handle non-finite values.
Results may differ from a plain program's by a relative error of at most 0.0034.
Values may be sent and summed in bfloat16 or wider, within the bound.
A program may use at most 64 MiB of HBM per device.

v0:
```python
import jax
import jax.numpy as jnp
from jax import lax
from jax.sharding import Mesh
from jax.sharding import PartitionSpec as P

STATE = 128
HEADDIM = 64
ADAPTER_EXPERTS = 16
EXPERT_RANK = 8
GROUP = 256
INNER_WIDTH = 3072
SEQ = ("seq_0", "seq_1")
SEQ_EXP = ("seq_0", "seq_1", "exp")
HIGH = lax.Precision.HIGHEST


def laid_out(parts, dim):
    lengths = list(parts.shape[1:])
    lengths[dim] *= parts.shape[0]
    return jnp.moveaxis(parts, 0, dim).reshape(lengths)


def copy_for_each(value, axis):
    size = lax.axis_size(axis)
    return lax.all_to_all(
        jnp.broadcast_to(value[None], (size, *value.shape)), axis, 0, 0, tiled=True
    )


def gathered_copies(value, axis, dim):
    return laid_out(copy_for_each(value, axis), dim)


def passed_along(block, axis, distance):
    devices = range(lax.axis_size(axis))
    route = [(i - distance, i) for i in devices if i - distance in devices]
    return lax.ppermute(block, axis, route)


def filled_with(value, identity):
    return jax.tree.map(
        lambda a, e: jnp.broadcast_to(jnp.asarray(e, a.dtype), a.shape), value, identity
    )


def entering_2(value, axes, combine, identity):
    before = start = filled_with(value, identity)
    running = value
    for axis in reversed(axes):
        size, index = (lax.axis_size(axis), lax.axis_index(axis))
        pieces = jax.tree.map(lambda part: lax.all_gather(part, axis), running)
        inside, running = (start, start)
        for k in range(size):
            passed = k < index
            running = combine(running, jax.tree.map(lambda part: part[k], pieces))
            inside = jax.tree.map(lambda new, old: jnp.where(passed, new, old), running, inside)
        before = combine(inside, before)
    return before


def taken_together(value, axis):
    return copy_for_each(value, axis).sum(axis=0)


def block_step(state, items):
    inner, bmap, cmap, step, decay = items
    cumul = jnp.cumsum(decay, axis=0)
    length = decay.shape[0]
    rows = lax.broadcasted_iota(jnp.int32, (length, length), 0)
    cols = lax.broadcasted_iota(jnp.int32, (length, length), 1)
    causal = (rows >= cols)[:, :, None]
    differ = jnp.where(causal, cumul[:, None, :] - cumul[None, :, :], 0.0)
    segment = jnp.where(causal, jnp.exp(differ), 0.0)
    gram = jnp.dot(cmap, bmap.T, precision=HIGH)
    weights = gram[:, :, None] * segment * step[None, :, :]
    output = jnp.einsum("ijh,jhp->ihp", weights, inner, precision=HIGH)
    output = output + jnp.exp(cumul)[:, :, None] * jnp.einsum(
        "in,hnp->ihp", cmap, state, precision=HIGH
    )
    final = cumul[-1]
    carried = jnp.exp(final[None, :] - cumul) * step
    update = jnp.einsum("jn,jhp->hnp", bmap, carried[:, :, None] * inner, precision=HIGH)
    return (jnp.exp(final)[:, None, None] * state + update, output)


def run_blocks(inner, bmap, cmap, step, decay, state, block):
    total = inner.shape[0]
    count_blocks = total // block
    items = (
        inner.reshape(count_blocks, block, inner.shape[1], inner.shape[2]),
        bmap.reshape(count_blocks, block, bmap.shape[1]),
        cmap.reshape(count_blocks, block, cmap.shape[1]),
        step.reshape(count_blocks, block, step.shape[1]),
        decay.reshape(count_blocks, block, decay.shape[1]),
    )
    final, output = lax.scan(block_step, state, items)
    return (final, output.reshape(total, inner.shape[1], inner.shape[2]))


def causal_conv(extended, weights, bias):
    length = extended.shape[0] - weights.shape[0] + 1
    output = bias[None, :] + jnp.zeros((length, weights.shape[1]), jnp.float32)
    for shift_idx in range(weights.shape[0]):
        output = output + weights[shift_idx][None, :] * extended[shift_idx : shift_idx + length]
    return jax.nn.silu(output)


def pick_ranks(partial_columns, route, experts, width):
    column_expert = lax.broadcasted_iota(jnp.int32, (experts * width,), 0) // width
    masked = jnp.where(route[:, None] == column_expert[None, :], partial_columns, 0.0)
    return jnp.sum(masked.reshape(partial_columns.shape[0], experts, width), axis=1)


def lift_ranks(ranks, route, experts):
    width = ranks.shape[1]
    column_expert = lax.broadcasted_iota(jnp.int32, (experts * width,), 0) // width
    repeated_tiles = jnp.tile(ranks, (1, experts))
    return jnp.where(
        route[:, None] == column_expert[None, :], repeated_tiles, jnp.zeros_like(repeated_tiles)
    )


def body(
    tokens,
    routes,
    gate_inner_weight,
    state_map_weight,
    step_size_weight,
    adapter_down_weight,
    adapter_up_weight,
    inner_conv_taps,
    state_map_taps,
    inner_conv_bias,
    state_map_conv_bias,
    step_size_bias,
    head_decay_rate,
    direct_head_scale,
    gated_norm_scale,
):
    whole, route_all = (
        lax.all_gather(tokens, "exp", axis=0, tiled=True),
        lax.all_gather(routes, "exp", axis=0, tiled=True),
    )
    route_flat = route_all[:, 0]
    all_down_maps = gathered_copies(adapter_down_weight, "exp", 1)
    partial_columns = jnp.dot(whole, all_down_maps, preferred_element_type=jnp.float32)
    ranks = pick_ranks(partial_columns, route_flat, ADAPTER_EXPERTS, EXPERT_RANK).astype(
        jnp.bfloat16
    )
    length = whole.shape[0]
    features = whole.shape[1]
    split_widths = gate_inner_weight.shape[2]
    raised_values = lift_ranks(ranks, route_flat, ADAPTER_EXPERTS)
    gate_inner_values = jnp.dot(
        whole,
        gate_inner_weight.reshape(features, 2 * split_widths),
        preferred_element_type=jnp.float32,
    )
    gate_inner_values = gate_inner_values + jnp.dot(
        raised_values,
        adapter_up_weight.reshape(ADAPTER_EXPERTS * EXPERT_RANK, 2 * split_widths),
        preferred_element_type=jnp.float32,
    )
    gate = gate_inner_values[:, :split_widths]
    inner = gate_inner_values[:, split_widths:]
    bc_raw = jnp.dot(whole, state_map_weight, preferred_element_type=jnp.float32)
    dt_raw = jnp.dot(whole, step_size_weight, preferred_element_type=jnp.float32)
    margin = inner_conv_taps.shape[0] - 1
    inner_rim, bc_rim = passed_along((inner[length - margin :], bc_raw[length - margin :]), SEQ, 1)
    xconv = causal_conv(
        jnp.concatenate([inner_rim, inner], axis=0), inner_conv_taps, inner_conv_bias
    )
    bconv = causal_conv(
        jnp.concatenate([bc_rim, bc_raw], axis=0), state_map_taps, state_map_conv_bias
    )
    bmap = bconv[:, :STATE]
    cmap = bconv[:, STATE:]
    step = jax.nn.softplus(dt_raw + step_size_bias[None, :])
    decay = -head_decay_rate[None, :] * step
    heads = head_decay_rate.shape[0]
    heads_in = xconv.reshape(length, heads, HEADDIM)
    empty_state = jnp.zeros((heads, STATE, HEADDIM), jnp.float32)
    final, output = run_blocks(heads_in, bmap, cmap, step, decay, empty_state, GROUP)
    factor = jnp.exp(jnp.sum(decay, axis=0))

    def combine(earlier, later):
        return (earlier[0] * later[0], later[0][:, None, None] * earlier[1] + later[1])

    total_decay, entering = entering_2(
        (factor, final), SEQ, combine, (jnp.ones((heads,), jnp.float32), empty_state)
    )
    cumul = jnp.cumsum(decay, axis=0)
    output = output + jnp.exp(cumul)[:, :, None] * jnp.einsum(
        "in,hnp->ihp", cmap, entering, precision=HIGH
    )
    output = output + direct_head_scale[None, :, None] * heads_in
    gated = output.reshape(length, split_widths) * jax.nn.silu(gate)
    squares = taken_together(jnp.sum(gated * gated, axis=1), "exp")
    scale = lax.rsqrt(squares / INNER_WIDTH + 1e-05)
    return (gated * scale[:, None] * gated_norm_scale[None, :]).astype(jnp.bfloat16)


def solution(mesh):
    split = Mesh(mesh.devices.reshape(8, 4, mesh.shape["exp"]), ("seq_0", "seq_1", "exp"))
    in_specs = (
        P(SEQ_EXP, None),
        P(SEQ_EXP, None),
        P(None, None, "exp"),
        P(),
        P(None, "exp"),
        P(None, "exp"),
        P(None, None, "exp"),
        P(None, "exp"),
        P(),
        P("exp"),
        P(),
        P("exp"),
        P("exp"),
        P("exp"),
        P("exp"),
    )
    out_specs = P(SEQ, "exp")
    return jax.shard_map(body, mesh=split, in_specs=in_specs, out_specs=out_specs, check_vma=False)
```

profile of v0, /device:TPU:1, one launch (start us, length us, event | category | flops | bytes accessed | tf_op | source)
XLA Modules:
  0.0 258.2 jit_solution(6099084624724914850)
XLA Ops:
  6.5 0.7 all-gather.6.cloned.1.call-update
  7.3 1.8 broadcast_in_dim.72
  9.0 6.6 %all-to-all-start = ((bf16[8,2560,16]{1,2,0:T(8,128)(2,1)}), bf16[8,2560,16]{1,2,0:T(8,128)(2,1)S(1)}, u32[]{:S(2)}, u32[]{:S(2)}) async-start(bf16[8,2560,16]{1,2,0:T(8,128)(2,1)} %broadcast_in_dim.72), calls=%async_computation | async-start | bytes 1310720 | tf_op jit(solution)/shard_map/all_to_all | solution.py:26
  15.7 4.8 %copy.123 = bf16[320,8,2,384]{3,1,2,0:T(8,128)(2,1)} copy(bf16[320,8,2,384]{3,2,1,0:T(2,128)(2,1)} %bitcast.267) | data formatting | bytes 7864320
  21.8 11.0 %all_gather.25 = s32[1024,1]{0,1:T(1,128)S(1)} all-gather(s32[128,1]{0,1:T(1,128)S(1)} %copy-done.18), channel_id=1, replica_groups=mesh['seq_0'=8,'seq_1'=4,'exp'=8] {'exp'}, dimensions={0}, use_global_device_ids=true | all-gather | bytes 4608 | tf_op jit(solution)/shard_map/all_gather | solution.py:143
  32.9 19.5 %all-gather.6.cloned.1.call-done = bf16[1024,2560]{1,0:T(8,128)(2,1)} async-done(((bf16[128,2560]{1,0:T(8,128)(2,1)}), bf16[1024,2560]{1,0:T(8,128)(2,1)}) %all-gather.6.cloned.1.call-update) | async-done | bytes 5242896 | tf_op jit(solution)/shard_map/all_gather | solution.py:142
  52.4 9.5 %fusion.98 = f32[1024,768]{1,0:T(8,128)} fusion(bf16[1024,2560]{1,0:T(8,128)(2,1)} %all-gather.6.cloned.1.call-done, bf16[2560,768]{1,0:T(8,128)(2,1)} %bitcast.268), kind=kOutput, calls=%fused_computation.167 | convolution fusion | flops 4026531840 | bytes 12320768 | tf_op jit(solution)/shard_map/dot_general | solution.py:155
  61.9 4.4 %fusion.54 = bf16[1024,8]{0,1:T(8,128)(2,1)S(1)} fusion(bf16[1024,2560]{1,0:T(8,128)(2,1)} %all-gather.6.cloned.1.call-done, bf16[2560,128]{0,1:T(8,128)(2,1)S(1)} %bitcast.271, s32[1024]{0:T(1024)S(1)} %bitcast.281, s32[128]{0:T(128)S(1)} %and_select_fusion), kind=kOutput, calls=%fused_computation.70 | convolution fusion | flops 671473664 | bytes 5919232 | tf_op jit(solution)/shard_map/dot_general | solution.py:147
  66.4 0.7 convolution_add_fusion
  67.1 1.6 copy-done.3
  68.8 3.2 %collective-permute-start = (f32[3,384]{1,0:T(4,128)S(1)}, f32[3,384]{1,0:T(4,128)S(1)}, u32[]{:S(2)}, u32[]{:S(2)}) collective-permute-start(f32[3,384]{1,0:T(4,128)S(1)} %slice.215), channel_id=1, source_target_pairs={{0,8},{8,16},{16,24},{24,32},{32,40},{40,48},{48,56},{56,64},{64,7... | collective-permute-start | bytes 13832 | tf_op jit(solution)/shard_map/ppermute | solution.py:38
  72.0 1.5 fusion.99
  73.6 3.1 %collective-permute-start.1 = (f32[3,256]{1,0:T(4,128)S(1)}, f32[3,256]{1,0:T(4,128)S(1)}, u32[]{:S(2)}, u32[]{:S(2)}) collective-permute-start(f32[3,256]{1,0:T(4,128)S(1)} %slice.221), channel_id=1, source_target_pairs={{0,8},{8,16},{16,24},{24,32},{32,40},{40,48},{48,56},{56,64},{64,7... | collective-permute-start | bytes 9224 | tf_op jit(solution)/shard_map/ppermute | solution.py:38
  76.7 1.6 fusion.95
  78.4 8.6 %all-reduce = f32[24]{0:T(128)S(1)} all-reduce(f32[24]{0:T(128)S(1)} %exponential_dynamic-update-slice_fusion), channel_id=2, replica_groups=mesh['seq_0'=8,'seq_1'=4,'exp'=8] {'seq_1'}, use_global_device_ids=true, to_apply=%add | all-reduce | flops 24 | bytes 192
  87.1 0.7 copy-done.16
  87.8 0.7 divide_multiply_fusion.1
  88.4 1.0 copy-done.5
  89.4 1.1 fusion.96
  90.5 0.7 slice-done
  91.2 2.2 divide_multiply_fusion
  93.4 1.9 copy.104
  95.3 1.9 reshape_reshape.3
  97.2 81.9 %while.13 = (s32[]{:T(128)}, f32[6,128,64]{1,2,0:T(8,128)S(1)}, f32[4,256,6,64]{1,0,3,2:T(4,128)}, f32[4,256,6]{1,2,0:T(8,128)S(1)}, f32[4,256,6]{1,2,0:T(8,128)...) while((s32[]{:T(128)}, f32[6,128,64]{1,2,0:T(8,128)S(1)}, ...), condition=%wide.region_4.5_spmd.clone, body=%wide.region_1.4_spmd.clone.sunk | while | flops 707316736 | bytes 6607687 | solution.py:97
  97.2 1.8 reduce-window.26
  99.7 1.4 fusion.133
  101.1 1.4 fusion.132
  102.5 1.8 constant_dynamic-slice_fusion.2
  104.3 2.0 fusion.134
  106.7 9.5 %dynamic_update_slice.6 = f32[4,256,6,64]{1,0,3,2:T(4,128)} dynamic-update-slice(f32[4,256,6,64]{1,0,3,2:T(4,128)} %get-tuple-element.250, f32[1,256,6,64]{1,0,3,2:T(1,128)S(1)} %copy.158, s32[]{:T(128)} %get-tuple-element.248, s32[]{:T(128)} %constant.71.clone.1..sunk, s32[]{:T(128)} %constant.71.clone.1..sunk, s32[]{:T(128)} %constant.71.clone.1..sunk) | dynamic-update-slice | bytes 786436 | tf_op jit(solution)/shard_map/while/body/jit(dynamic_update_index_in_dim)/dynamic_update_slice | solution.py:97
  116.2 1.4 fusion.131
  117.7 1.8 reduce-window.26
  120.2 1.4 fusion.133
  121.6 1.3 fusion.132
  122.9 1.8 constant_dynamic-slice_fusion.2
  124.8 2.0 fusion.134
  127.2 9.5 %dynamic_update_slice.6 = f32[4,256,6,64]{1,0,3,2:T(4,128)} dynamic-update-slice(f32[4,256,6,64]{1,0,3,2:T(4,128)} %get-tuple-element.250, f32[1,256,6,64]{1,0,3,2:T(1,128)S(1)} %copy.158, s32[]{:T(128)} %get-tuple-element.248, s32[]{:T(128)} %constant.71.clone.1..sunk, s32[]{:T(128)} %constant.71.clone.1..sunk, s32[]{:T(128)} %constant.71.clone.1..sunk) | dynamic-update-slice | bytes 786436 | tf_op jit(solution)/shard_map/while/body/jit(dynamic_update_index_in_dim)/dynamic_update_slice | solution.py:97
  136.7 1.4 fusion.131
  138.1 1.8 reduce-window.26
  140.7 1.4 fusion.133
  142.1 1.4 fusion.132
  143.4 1.8 constant_dynamic-slice_fusion.2
  145.3 2.0 fusion.134
  147.7 9.5 %dynamic_update_slice.6 = f32[4,256,6,64]{1,0,3,2:T(4,128)} dynamic-update-slice(f32[4,256,6,64]{1,0,3,2:T(4,128)} %get-tuple-element.250, f32[1,256,6,64]{1,0,3,2:T(1,128)S(1)} %copy.158, s32[]{:T(128)} %get-tuple-element.248, s32[]{:T(128)} %constant.71.clone.1..sunk, s32[]{:T(128)} %constant.71.clone.1..sunk, s32[]{:T(128)} %constant.71.clone.1..sunk) | dynamic-update-slice | bytes 786436 | tf_op jit(solution)/shard_map/while/body/jit(dynamic_update_index_in_dim)/dynamic_update_slice | solution.py:97
  157.2 1.4 fusion.131
  158.6 1.8 reduce-window.26
  161.1 1.4 fusion.133
  162.5 1.3 fusion.132
  163.9 1.8 constant_dynamic-slice_fusion.2
  165.7 2.0 fusion.134
  168.1 9.5 %dynamic_update_slice.6 = f32[4,256,6,64]{1,0,3,2:T(4,128)} dynamic-update-slice(f32[4,256,6,64]{1,0,3,2:T(4,128)} %get-tuple-element.250, f32[1,256,6,64]{1,0,3,2:T(1,128)S(1)} %copy.158, s32[]{:T(128)} %get-tuple-element.248, s32[]{:T(128)} %constant.71.clone.1..sunk, s32[]{:T(128)} %constant.71.clone.1..sunk, s32[]{:T(128)} %constant.71.clone.1..sunk) | dynamic-update-slice | bytes 786436 | tf_op jit(solution)/shard_map/while/body/jit(dynamic_update_index_in_dim)/dynamic_update_slice | solution.py:97
  177.6 1.4 fusion.131
  179.0 11.5 %all-gather.1 = f32[24,128,64]{1,2,0:T(8,128)S(1)} all-gather(f32[6,128,64]{1,2,0:T(8,128)S(1)} %get-tuple-element.49), channel_id=3, replica_groups=mesh['seq_0'=8,'seq_1'=4,'exp'=8] {'seq_1'}, dimensions={0}, use_global_device_ids=true | all-gather | bytes 983040 | tf_op jit(solution)/shard_map/all_gather | solution.py:52
  190.6 0.8 bitcast_add_fusion
  191.5 1.7 reduce-window.16
  193.6 12.4 %all-gather.2 = f32[8,1,6]{2,1,0:T(1,128)S(1)} all-gather(f32[1,1,6]{2,1,0:T(1,128)S(1)} %get-tuple-element.177), channel_id=1, replica_groups=mesh['seq_0'=8,'seq_1'=4,'exp'=8] {'seq_0'}, dimensions={0}, use_global_device_ids=true | all-gather | bytes 216 | tf_op jit(solution)/shard_map/all_gather | solution.py:52
  206.0 2.9 %reshape.225 = f32[1024,6,64]{0,2,1:T(8,128)} reshape(f32[4,256,6,64]{1,0,3,2:T(4,128)} %get-tuple-element.48) | data formatting | bytes 3145728 | tf_op jit(solution)/shard_map/reshape | solution.py:98
  208.9 19.9 %all-gather.8.cloned.1.call-done = f32[8,6,128,64]{2,3,1,0:T(8,128)} async-done(((f32[1,6,128,64]{2,3,1,0:T(8,128)}), f32[8,6,128,64]{2,3,1,0:T(8,128)}) %all-gather.8.cloned.1.call-update) | async-done | bytes 1572880 | tf_op jit(solution)/shard_map/all_gather | solution.py:52
  228.8 2.0 fusion.71
  230.8 1.4 fusion.93
  232.8 1.6 copy.110
  234.5 2.5 multiply_reduce_fusion
  236.9 13.3 %all_to_all.11 = f32[8,1,1024]{2,1,0:T(1,128)S(1)} all-to-all(f32[8,1,1024]{2,1,0:T(1,128)S(1)} %broadcast_in_dim.77), channel_id=1, replica_groups=mesh['seq_0'=8,'seq_1'=4,'exp'=8] {'exp'}, dimensions={0} | all-to-all | bytes 65536 | tf_op jit(solution)/shard_map/all_to_all | solution.py:26
  250.3 1.1 multiply_convert_fusion
  (131 shorter events, 6.6 us)
Async XLA Ops:
  6.5 65.5 %copy-start = (bf16[2560,256]{1,0:T(8,128)(2,1)S(1)}, bf16[2560,256]{1,0:T(8,128)(2,1)}, u32[]{:S(2)}) copy-start(bf16[2560,256]{1,0:T(8,128)(2,1)} %param.20) | copy-start | bytes 3932164
  6.5 45.9 %all-gather.6.cloned.1.call-start = ((), (), s32[]{:S(2)}) async-start(), calls=%async_computation.2 | async-start | bytes 5898240 | tf_op jit(solution)/shard_map/all_gather | solution.py:142
  9.0 52.9 %all-to-all-start = ((bf16[8,2560,16]{1,2,0:T(8,128)(2,1)}), bf16[8,2560,16]{1,2,0:T(8,128)(2,1)S(1)}, u32[]{:S(2)}, u32[]{:S(2)}) async-start(bf16[8,2560,16]{1,2,0:T(8,128)(2,1)} %broadcast_in_dim.72), calls=%async_computation | async-start | bytes 1310720 | tf_op jit(solution)/shard_map/all_to_all | solution.py:26
  15.7 213.2 %all-gather.8.cloned.1.call-start = ((), (), s32[]{:S(2)}) async-start(), calls=%async_computation.3 | async-start | bytes 1769472 | tf_op jit(solution)/shard_map/all_gather | solution.py:52
  15.7 4.9 %copy-start.9 = (bf16[128,2,384]{2,1,0:T(2,128)(2,1)S(1)}, bf16[128,2,384]{2,1,0:T(2,128)(2,1)}, u32[]{:S(2)}) copy-start(bf16[128,2,384]{2,1,0:T(2,128)(2,1)} %param.23) | copy-start | bytes 589828
  15.7 4.9 %copy-start.19 = (f32[6]{0:T(128)S(1)}, f32[6]{0:T(128)}, u32[]{:S(2)}) copy-start(f32[6]{0:T(128)} %param.29) | copy-start | bytes 76
  15.7 5.0 %copy-start.20 = (u32[256]{0:T(256)S(1)}, u32[256]{0:T(256)}, u32[]{:S(2)}) copy-start(u32[256]{0:T(256)} %constant.97) | copy-start | bytes 3076
  15.7 6.1 %copy-start.18 = (s32[128,1]{0,1:T(1,128)S(1)}, s32[128,1]{0,1:T(1,128)}, u32[]{:S(2)}) copy-start(s32[128,1]{0,1:T(1,128)} %param.18) | copy-start | bytes 1540
  15.7 17.1 %copy-start.11 = (f32[4,384]{1,0:T(4,128)S(1)}, f32[4,384]{1,0:T(4,128)}, u32[]{:S(2)}) copy-start(f32[4,384]{1,0:T(4,128)} %param.24) | copy-start | bytes 18436
  15.7 17.1 %copy-start.12 = (f32[4,256]{1,0:T(4,128)S(1)}, f32[4,256]{1,0:T(4,128)}, u32[]{:S(2)}) copy-start(f32[4,256]{1,0:T(4,128)} %param.25) | copy-start | bytes 12292
  61.9 4.4 %copy-start.8 = (f32[1024,768]{1,0:T(8,128)S(1)}, f32[1024,768]{1,0:T(8,128)}, u32[]{:S(2)}) copy-start(f32[1024,768]{1,0:T(8,128)} %fusion.98) | copy-start | bytes 9437188
  66.4 5.6 %copy-start.4 = (bf16[1024,2560]{1,0:T(8,128)(2,1)S(1)}, bf16[1024,2560]{1,0:T(8,128)(2,1)}, u32[]{:S(2)}) copy-start(bf16[1024,2560]{1,0:T(8,128)(2,1)} %all-gather.6.cloned.1.call-done) | copy-start | bytes 15728644
  67.1 1.7 copy-start.3
  68.8 7.9 %copy-start.10 = (bf16[2560,6]{0,1:T(8,128)(2,1)S(1)}, bf16[2560,6]{0,1:T(8,128)(2,1)}, u32[]{:S(2)}) copy-start(bf16[2560,6]{0,1:T(8,128)(2,1)} %param.21) | copy-start | bytes 92164
  68.8 7.9 %copy-start.14 = (f32[6]{0:T(128)S(1)}, f32[6]{0:T(128)}, u32[]{:S(2)}) copy-start(f32[6]{0:T(128)} %param.28) | copy-start | bytes 76
  68.8 21.7 %collective-permute-start = (f32[3,384]{1,0:T(4,128)S(1)}, f32[3,384]{1,0:T(4,128)S(1)}, u32[]{:S(2)}, u32[]{:S(2)}) collective-permute-start(f32[3,384]{1,0:T(4,128)S(1)} %slice.215), channel_id=1, source_target_pairs={{0,8},{8,16},{16,24},{24,32},{32,40},{40,48},{48,56},{56,64},{64,7... | collective-permute-start | bytes 13832 | tf_op jit(solution)/shard_map/ppermute | solution.py:38
  73.6 13.5 %collective-permute-start.1 = (f32[3,256]{1,0:T(4,128)S(1)}, f32[3,256]{1,0:T(4,128)S(1)}, u32[]{:S(2)}, u32[]{:S(2)}) collective-permute-start(f32[3,256]{1,0:T(4,128)S(1)} %slice.221), channel_id=1, source_target_pairs={{0,8},{8,16},{16,24},{24,32},{32,40},{40,48},{48,56},{56,64},{64,7... | collective-permute-start | bytes 9224 | tf_op jit(solution)/shard_map/ppermute | solution.py:38
  87.1 0.7 copy-start.16
  88.4 1.0 copy-start.5
  89.4 1.8 slice-start
  89.4 1.8 copy-start.13
  95.3 1.9 copy-start.1
  208.9 21.9 %copy-start.6 = (f32[1024,256]{1,0:T(8,128)S(1)}, f32[1024,256]{1,0:T(8,128)}, u32[]{:S(2)}) copy-start(f32[1024,256]{1,0:T(8,128)} %copy-done.5) | copy-start | bytes 3145732
  228.8 3.4 %copy-start.7 = (f32[1024,6,64]{0,2,1:T(8,128)S(1)}, f32[1024,6,64]{0,2,1:T(8,128)}, u32[]{:S(2)}) copy-start(f32[1024,6,64]{0,2,1:T(8,128)} %reshape.225) | copy-start | bytes 4718596
  230.8 1.5 copy-start.2
  230.8 1.5 copy-start.17
  234.5 15.8 %copy-start.15 = (f32[384]{0:T(512)S(1)}, f32[384]{0:T(512)}, u32[]{:S(2)}) copy-start(f32[384]{0:T(512)} %param.31) | copy-start | bytes 4612
Sparse Core Ops, SparseCore 0:
  9.2 43.2 all-gather.5
  191.5 37.2 all-gather.7
where the time goes:
time: 260 us; the launch traced here: 258 us
  local copies, waits for them, and re-layouts  69.9 us (27%)
  blocking collectives  56.9 us (22%)
  matrix products  43.5 us (17%)
  waiting for transfers between devices  40.2 us (15%)
  other arithmetic  20.2 us (8%)
  between operations  14.4 us (6%)
  starting transfers between devices  13 us (5%)
    dynamic_update_slice x8, local copies, waits for them, and re-layouts, run_blocks(): final, output = lax.scan(block_step, state, items)  39.7 us
    all_gather x2, blocking collectives, entering_2(): pieces = jax.tree.map(lambda part: lax.all_gather(part, axis), running)  23.9 us
    all_gather x1, waiting for transfers between devices, entering_2(): pieces = jax.tree.map(lambda part: lax.all_gather(part, axis), running)  19.9 us
    all_gather x1, waiting for transfers between devices, body(): lax.all_gather(tokens, 'exp', axis=0, tiled=True)  19.5 us
    all_to_all x1, blocking collectives, copy_for_each(): lax.all_to_all(jnp.broadcast_to(value[None], (size, *value.shape)), axis,...  13.3 us
    all_gather x1, blocking collectives, body(): lax.all_gather(routes, 'exp', axis=0, tiled=True)  11 us
    dot_general x1, matrix products, body(): jnp.dot(whole, gate_inner_weight.reshape(features, 2 * split_widths), pre...  9.51 us
    another operation x10, other arithmetic  9.32 us
  transfers between devices with their start and end apart: 5, of which 2 were waited for; matrix products, arithmetic and copies ran while one was open for 10% of the time, Pallas kernels for 0%

commit v1 on v0

--- a/solution.py
+++ b/solution.py
@@ -13,6 +13,27 @@
 SEQ = ("seq_0", "seq_1")
 SEQ_EXP = ("seq_0", "seq_1", "exp")
 HIGH = lax.Precision.HIGHEST
+
+
+def gather_around(value, axis, dim):
+    size, mine, extent = (lax.axis_size(axis), lax.axis_index(axis), value.shape[dim])
+    upward = [(i, (i + 1) % size) for i in range(size)]
+    left = [(i, (i - 1) % size) for i in range(size)]
+    whole = jnp.zeros((*value.shape[:dim], size * extent, *value.shape[dim + 1 :]), value.dtype)
+    whole = lax.dynamic_update_slice_in_dim(whole, value, mine * extent, axis=dim)
+    from_left = from_right = value
+    half = size // 2
+    for step in range(1, half + 1):
+        from_left = lax.ppermute(from_left, axis, upward)
+        whole = lax.dynamic_update_slice_in_dim(
+            whole, from_left, (mine - step) % size * extent, axis=dim
+        )
+        if step < size - half:
+            from_right = lax.ppermute(from_right, axis, left)
+            whole = lax.dynamic_update_slice_in_dim(
+                whole, from_right, (mine + step) % size * extent, axis=dim
+            )
+    return whole
 
 
 def laid_out(parts, dim):
@@ -139,7 +160,7 @@
     gated_norm_scale,
 ):
     whole, route_all = (
-        lax.all_gather(tokens, "exp", axis=0, tiled=True),
+        gather_around(tokens, "exp", 0),
         lax.all_gather(routes, "exp", axis=0, tiled=True),
     )
     route_flat = route_all[:, 0]

time: 260 us -> 301 us (1.16)
  local copies, waits for them, and re-layouts: 69.9 us -> 84.9 us
  other arithmetic: 20.2 us -> 29.3 us
  starting transfers between devices: 13 us -> 20.9 us
  blocking collectives: 56.9 us -> 62.7 us
    all_gather x1 -> x0, waiting for transfers between devices: 19.5 us -> none  [body(): lax.all_gather(tokens, 'exp', axis=0, tiled=True)]
    ppermute x0 -> x7, waiting for transfers between devices: none -> 14.7 us  [the longest x4 14.6 us: gather_around(): from_left = lax.ppermute(from_left, axis, upward)]
    ppermute x0 -> x7, starting transfers between devices: none -> 9.84 us  [the longest x4 7.53 us: gather_around(): from_left = lax.ppermute(from_left, axis, upward)]
    dynamic_update_slice x0 -> x8, local copies, waits for them, and re-layouts: none -> 8.2 us  [the longest x4 4.65 us: gather_around(): lax.dynamic_update_slice_in_dim(whole, from_left, (mine - step) % size *...]
    all_gather x1, waiting for transfers between devices: 19.9 us -> 25.6 us  [entering_2(): pieces = jax.tree.map(lambda part: lax.all_gather(part, axis), running)]
    all_gather x1, blocking collectives: 11 us -> 15.9 us  [body(): lax.all_gather(routes, 'exp', axis=0, tiled=True)]
    dot_general x1, matrix products: 9.51 us -> 6.16 us  [body(): jnp.dot(whole, gate_inner_weight.reshape(features, 2 * split_widths), pre...]
    dot_general x1, matrix products: 1.59 us -> 4.67 us  [body(): jnp.dot(whole, step_size_weight, preferred_element_type=jnp.float32)]
  transfers between devices with their start and end apart: 5 -> 11, of which waited for: 2 -> 5; matrix products, arithmetic and copies ran while one was open for 10% -> 11% of each run, Pallas kernels for 0% -> 0%
where the time goes in v1:
time: 301 us; the launch traced here: 299 us
  local copies, waits for them, and re-layouts  84.9 us (28%)
  blocking collectives  62.7 us (21%)
  matrix products  45.7 us (15%)
  waiting for transfers between devices  40.3 us (13%)
  other arithmetic  29.3 us (10%)
  starting transfers between devices  20.9 us (7%)
  between operations  14.7 us (5%)
    dynamic_update_slice x8, local copies, waits for them, and re-layouts, run_blocks(): final, output = lax.scan(block_step, state, items)  39.7 us
    all_gather x1, waiting for transfers between devices, entering_2(): pieces = jax.tree.map(lambda part: lax.all_gather(part, axis), running)  25.6 us
    all_gather x2, blocking collectives, entering_2(): pieces = jax.tree.map(lambda part: lax.all_gather(part, axis), running)  24.5 us
    all_gather x1, blocking collectives, body(): lax.all_gather(routes, 'exp', axis=0, tiled=True)  15.9 us
    ppermute x4, waiting for transfers between devices, gather_around(): from_left = lax.ppermute(from_left, axis, upward)  14.6 us
    all_to_all x1, blocking collectives, copy_for_each(): lax.all_to_all(jnp.broadcast_to(value[None], (size, *value.shape)), axis,...  13.3 us
    another operation x10, other arithmetic  11.7 us
    unnamed x1, blocking collectives  8.96 us
  transfers between devices with their start and end apart: 11, of which 5 were waited for; matrix products, arithmetic and copies ran while one was open for 11% of the time, Pallas kernels for 0%

profile of v1, /device:TPU:1, one launch (start us, length us, event | category | flops | bytes accessed | tf_op | source)
XLA Modules:
  0.0 298.9 jit_solution(10646274630234138494)
XLA Ops:
  6.5 2.7 collective-permute-start
  9.8 1.8 broadcast_in_dim.76
  11.5 6.4 %all-to-all-start = ((bf16[8,2560,16]{1,2,0:T(8,128)(2,1)}), bf16[8,2560,16]{1,2,0:T(8,128)(2,1)S(1)}, u32[]{:S(2)}, u32[]{:S(2)}) async-start(bf16[8,2560,16]{1,2,0:T(8,128)(2,1)} %broadcast_in_dim.76), calls=%async_computation | async-start | bytes 1310720 | tf_op jit(solution)/shard_map/all_to_all | solution.py:47
  18.1 15.9 %all_gather.21 = s32[1024,1]{0,1:T(1,128)S(1)} all-gather(s32[128,1]{0,1:T(1,128)S(1)} %copy-done.29), channel_id=1, replica_groups=mesh['seq_0'=8,'seq_1'=4,'exp'=8] {'exp'}, dimensions={0}, use_global_device_ids=true | all-gather | bytes 4608 | tf_op jit(solution)/shard_map/all_gather | solution.py:164
  34.0 4.7 %copy.123 = bf16[320,8,2,384]{3,1,2,0:T(8,128)(2,1)} copy(bf16[320,8,2,384]{3,2,1,0:T(2,128)(2,1)} %bitcast.267) | data formatting | bytes 7864320
  40.2 2.6 broadcast_in_dim.75
  44.3 2.0 constant_dynamic-update-slice_fusion.6
  47.1 4.5 %collective-permute-done.2 = bf16[128,2560]{1,0:T(8,128)(2,1)S(1)} collective-permute-done((bf16[128,2560]{1,0:T(8,128)(2,1)}, bf16[128,2560]{1,0:T(8,128)(2,1)S(1)}, u32[]{:S(2)}, u32[]{:S(2)}) %collective-permute-start.2) | collective-permute-done | bytes 655392 | tf_op jit(solution)/shard_map/ppermute | solution.py:27
  51.6 2.4 collective-permute-start.4
  57.1 4.4 %collective-permute-done.4 = bf16[128,2560]{1,0:T(8,128)(2,1)S(1)} collective-permute-done((bf16[128,2560]{1,0:T(8,128)(2,1)S(1)}, bf16[128,2560]{1,0:T(8,128)(2,1)S(1)}, u32[]{:S(2)}, u32[]{:S(2)}) %collective-permute-start.4) | collective-permute-done | bytes 655392 | tf_op jit(solution)/shard_map/ppermute | solution.py:27
  61.5 2.5 collective-permute-start.6
  65.8 5.7 %collective-permute-done.6 = bf16[128,2560]{1,0:T(8,128)(2,1)S(1)} collective-permute-done((bf16[128,2560]{1,0:T(8,128)(2,1)S(1)}, bf16[128,2560]{1,0:T(8,128)(2,1)S(1)}, u32[]{:S(2)}, u32[]{:S(2)}) %collective-permute-start.6) | collective-permute-done | bytes 655392 | tf_op jit(solution)/shard_map/ppermute | solution.py:27
  72.4 4.4 %fusion.54 = bf16[1024,8]{0,1:T(8,128)(2,1)S(1)} fusion(bf16[1024,2560]{1,0:T(8,128)(2,1)} %constant_dynamic-update-slice_fusion, bf16[2560,128]{0,1:T(8,128)(2,1)S(1)} %bitcast.271, s32[1024]{0:T(1024)S(1)} %bitcast.280, s32[128]{0:T(128)S(1)} %and_select_fusion), kind=kOutput, calls=%fused_computation.70 | convolution fusion | flops 671473664 | bytes 5919232 | tf_op jit(solution)/shard_map/dot_general | solution.py:168
  77.5 6.2 %convolution_add_fusion = f32[1024,768]{1,0:T(8,128)S(1)} fusion(f32[1024,768]{1,0:T(8,128)S(1)} %fusion.65, bf16[1024,2560]{1,0:T(8,128)(2,1)} %constant_dynamic-update-slice_fusion, bf16[2560,768]{1,0:T(8,128)(2,1)S(1)} %bitcast.268), kind=kOutput, calls=%fused_computation.50 | convolution fusion | flops 4027318272 | bytes 15466496 | tf_op jit(solution)/shard_map/dot_general | solution.py:176
  83.8 1.5 collective-permute-start.7
  85.3 4.0 %fusion.99 = f32[1024,256]{1,0:T(8,128)S(1)} fusion(bf16[1024,2560]{1,0:T(8,128)(2,1)} %constant_dynamic-update-slice_fusion, bf16[2560,256]{1,0:T(8,128)(2,1)S(1)} %copy-done), kind=kOutput, calls=%fused_computation.176 | convolution fusion | flops 1342177280 | bytes 7602176 | tf_op jit(solution)/shard_map/dot_general | solution.py:188
  89.3 3.1 %collective-permute-start.8 = (f32[3,256]{1,0:T(4,128)S(1)}, f32[3,256]{1,0:T(4,128)S(1)}, u32[]{:S(2)}, u32[]{:S(2)}) collective-permute-start(f32[3,256]{1,0:T(4,128)S(1)} %slice.221), channel_id=1, source_target_pairs={{0,8},{8,16},{16,24},{24,32},{32,40},{40,48},{48,56},{56,64},{64,7... | collective-permute-start | bytes 9224 | tf_op jit(solution)/shard_map/ppermute | solution.py:59
  92.5 4.7 %fusion.96 = (f32[6]{0:T(128)S(1)}, f32[1024,6]{0,1:T(8,128)S(1)}, f32[1024,6]{0,1:T(8,128)S(1)}, f32[1024,6]{0,1:T(8,128)}) fusion(f32[6]{0:T(128)S(1)} %neg.22, f32[6]{0:T(128)S(1)} %copy-done.23, bf16[1024,2560]{1,0:T(8,128)(2,1)} %constant_dynamic-update-slice_fusion, bf16[2560,6]{0,1:T(8,128)(2,1)S(1)} %copy-done.13), kind=kOutput, calls=%fused_computation.173 | convolution fusion | flops 31512570 | bytes 5347400 | tf_op jit(solution)/shard_map/dot_general | solution.py:189
  97.3 9.0 %all-reduce = f32[24]{0:T(128)S(1)} all-reduce(f32[24]{0:T(128)S(1)} %exponential_dynamic-update-slice_fusion), channel_id=2, replica_groups=mesh['seq_0'=8,'seq_1'=4,'exp'=8] {'seq_1'}, use_global_device_ids=true, to_apply=%add | all-reduce | flops 24 | bytes 192
  111.1 2.1 divide_multiply_fusion
  113.2 1.9 copy.104
  115.1 1.9 reshape_reshape.3
  117.0 91.1 %while.13 = (s32[]{:T(128)}, f32[6,128,64]{1,2,0:T(8,128)S(1)}, f32[4,256,6,64]{1,0,3,2:T(4,128)}, f32[4,256,6]{1,2,0:T(8,128)S(1)}, f32[4,256,6]{1,2,0:T(8,128)...) while((s32[]{:T(128)}, f32[6,128,64]{1,2,0:T(8,128)S(1)}, ...), condition=%wide.region_4.5_spmd.clone, body=%wide.region_1.4_spmd.clone.sunk | while | flops 707316736 | bytes 6656011 | solution.py:118
  117.0 1.8 constant_dynamic-slice_fusion.2
  118.8 1.8 reduce-window.26
  123.6 1.4 fusion.131
  125.0 1.3 fusion.132
  126.4 1.4 fusion.133
  127.8 2.0 fusion.134
  130.2 9.5 %dynamic_update_slice.46 = f32[4,256,6,64]{1,0,3,2:T(4,128)} dynamic-update-slice(f32[4,256,6,64]{1,0,3,2:T(4,128)} %get-tuple-element.250, f32[1,256,6,64]{1,0,3,2:T(1,128)S(1)} %copy.158, s32[]{:T(128)S(6)} %copy.171, s32[]{:T(128)} %constant.113.clone.1..sunk, s32[]{:T(128)} %constant.113.clone.1..sunk, s32[]{:T(128)} %constant.113.clone.1..sunk) | dynamic-update-slice | bytes 786436 | tf_op jit(solution)/shard_map/while/body/jit(dynamic_update_index_in_dim)/dynamic_update_slice | solution.py:118
  139.7 1.8 constant_dynamic-slice_fusion.2
  141.6 1.8 reduce-window.26
  146.4 1.4 fusion.131
  147.8 1.4 fusion.132
  149.2 1.4 fusion.133
  150.6 2.0 fusion.134
  153.0 9.5 %dynamic_update_slice.46 = f32[4,256,6,64]{1,0,3,2:T(4,128)} dynamic-update-slice(f32[4,256,6,64]{1,0,3,2:T(4,128)} %get-tuple-element.250, f32[1,256,6,64]{1,0,3,2:T(1,128)S(1)} %copy.158, s32[]{:T(128)S(6)} %copy.171, s32[]{:T(128)} %constant.113.clone.1..sunk, s32[]{:T(128)} %constant.113.clone.1..sunk, s32[]{:T(128)} %constant.113.clone.1..sunk) | dynamic-update-slice | bytes 786436 | tf_op jit(solution)/shard_map/while/body/jit(dynamic_update_index_in_dim)/dynamic_update_slice | solution.py:118
  162.5 1.8 constant_dynamic-slice_fusion.2
  164.4 1.8 reduce-window.26
  169.2 1.4 fusion.131
  170.6 1.3 fusion.132
  172.0 1.4 fusion.133
  173.4 2.0 fusion.134
  175.8 9.5 %dynamic_update_slice.46 = f32[4,256,6,64]{1,0,3,2:T(4,128)} dynamic-update-slice(f32[4,256,6,64]{1,0,3,2:T(4,128)} %get-tuple-element.250, f32[1,256,6,64]{1,0,3,2:T(1,128)S(1)} %copy.158, s32[]{:T(128)S(6)} %copy.171, s32[]{:T(128)} %constant.113.clone.1..sunk, s32[]{:T(128)} %constant.113.clone.1..sunk, s32[]{:T(128)} %constant.113.clone.1..sunk) | dynamic-update-slice | bytes 786436 | tf_op jit(solution)/shard_map/while/body/jit(dynamic_update_index_in_dim)/dynamic_update_slice | solution.py:118
  185.3 1.8 constant_dynamic-slice_fusion.2
  187.1 1.8 reduce-window.26
  192.0 1.4 fusion.131
  193.4 1.4 fusion.132
  194.8 1.4 fusion.133
  196.2 2.0 fusion.134
  198.5 9.5 %dynamic_update_slice.46 = f32[4,256,6,64]{1,0,3,2:T(4,128)} dynamic-update-slice(f32[4,256,6,64]{1,0,3,2:T(4,128)} %get-tuple-element.250, f32[1,256,6,64]{1,0,3,2:T(1,128)S(1)} %copy.158, s32[]{:T(128)S(6)} %copy.171, s32[]{:T(128)} %constant.113.clone.1..sunk, s32[]{:T(128)} %constant.113.clone.1..sunk, s32[]{:T(128)} %constant.113.clone.1..sunk) | dynamic-update-slice | bytes 786436 | tf_op jit(solution)/shard_map/while/body/jit(dynamic_update_index_in_dim)/dynamic_update_slice | solution.py:118
  208.1 10.6 %all-gather.1 = f32[24,128,64]{1,2,0:T(8,128)S(1)} all-gather(f32[6,128,64]{1,2,0:T(8,128)S(1)} %get-tuple-element.49), channel_id=3, replica_groups=mesh['seq_0'=8,'seq_1'=4,'exp'=8] {'seq_1'}, dimensions={0}, use_global_device_ids=true | all-gather | bytes 983040 | tf_op jit(solution)/shard_map/all_gather | solution.py:73
  219.5 1.5 bitcast_add_fusion
  221.1 1.7 reduce-window.16
  223.3 14.0 %all-gather.2 = f32[8,1,6]{2,1,0:T(1,128)S(1)} all-gather(f32[1,1,6]{2,1,0:T(1,128)S(1)} %copy-done.24), channel_id=1, replica_groups=mesh['seq_0'=8,'seq_1'=4,'exp'=8] {'seq_0'}, dimensions={0}, use_global_device_ids=true | all-gather | bytes 216 | tf_op jit(solution)/shard_map/all_gather | solution.py:73
  237.3 2.9 reshape.225
  240.2 25.6 %all-gather.5.cloned.1.call-done = f32[8,6,128,64]{2,3,1,0:T(8,128)} async-done(((f32[1,6,128,64]{2,3,1,0:T(8,128)}), f32[8,6,128,64]{2,3,1,0:T(8,128)}) %all-gather.5.cloned.1.call-update) | async-done | bytes 1572880 | tf_op jit(solution)/shard_map/all_gather | solution.py:73
  265.8 2.2 fusion.72
  268.0 1.4 fusion.94
  269.5 1.7 multiply_add_fusion
  271.2 1.9 copy.110
  273.1 3.1 %multiply_reduce_fusion = (f32[1024]{0:T(1024)S(1)}, f32[1024,384]{1,0:T(8,128)}) fusion(f32[1024,384]{1,0:T(8,128)S(1)} %copy.110, f32[1024,768]{1,0:T(8,128)} %copy-done.4), kind=kLoop, calls=%fused_computation.62 | loop fusion | flops 2751488 | bytes 4722688 | tf_op jit(solution)/shard_map/reduce_sum | solution.py:220
  276.2 13.3 %all_to_all.11 = f32[8,1,1024]{2,1,0:T(1,128)S(1)} all-to-all(f32[8,1,1024]{2,1,0:T(1,128)S(1)} %broadcast_in_dim.81), channel_id=1, replica_groups=mesh['seq_0'=8,'seq_1'=4,'exp'=8] {'exp'}, dimensions={0} | all-to-all | bytes 65536 | tf_op jit(solution)/shard_map/all_to_all | solution.py:47
  289.5 2.5 multiply_convert_fusion
  (191 shorter events, 30.2 us)
Async XLA Ops:
  6.5 78.8 %copy-start = (bf16[2560,256]{1,0:T(8,128)(2,1)S(1)}, bf16[2560,256]{1,0:T(8,128)(2,1)}, u32[]{:S(2)}) copy-start(bf16[2560,256]{1,0:T(8,128)(2,1)} %param.20) | copy-start | bytes 3932164
  6.5 11.5 %copy-start.10 = (bf16[128,2,384]{2,1,0:T(2,128)(2,1)S(1)}, bf16[128,2,384]{2,1,0:T(2,128)(2,1)}, u32[]{:S(2)}) copy-start(bf16[128,2,384]{2,1,0:T(2,128)(2,1)} %param.23) | copy-start | bytes 589828
  6.5 11.6 %copy-start.29 = (s32[128,1]{0,1:T(1,128)S(1)}, s32[128,1]{0,1:T(1,128)}, u32[]{:S(2)}) copy-start(s32[128,1]{0,1:T(1,128)} %param.18) | copy-start | bytes 1540
  6.5 37.2 %collective-permute-start = (bf16[128,2560]{1,0:T(8,128)(2,1)}, bf16[128,2560]{1,0:T(8,128)(2,1)}, u32[]{:S(2)}, u32[]{:S(2)}) collective-permute-start(bf16[128,2560]{1,0:T(8,128)(2,1)} %param.17), channel_id=1, source_target_pairs={{0,1},{1,2},{2,3},{3,4},{4,5},{5,6},{6,7},{7,0},{8,9},{9,10},{10,1... | collective-permute-start | bytes 1966088 | tf_op jit(solution)/shard_map/ppermute | solution.py:27
  9.2 34.5 %collective-permute-start.1 = (bf16[128,2560]{1,0:T(8,128)(2,1)}, bf16[128,2560]{1,0:T(8,128)(2,1)S(1)}, u32[]{:S(2)}, u32[]{:S(2)}) collective-permute-start(bf16[128,2560]{1,0:T(8,128)(2,1)} %param.17), channel_id=1, source_target_pairs={{0,7},{1,0},{2,1},{3,2},{4,3},{5,4},{6,5},{7,6},{8,15},{9,8},{10,9... | collective-permute-start | bytes 1966088 | tf_op jit(solution)/shard_map/ppermute | solution.py:32
  11.5 60.9 %all-to-all-start = ((bf16[8,2560,16]{1,2,0:T(8,128)(2,1)}), bf16[8,2560,16]{1,2,0:T(8,128)(2,1)S(1)}, u32[]{:S(2)}, u32[]{:S(2)}) async-start(bf16[8,2560,16]{1,2,0:T(8,128)(2,1)} %broadcast_in_dim.76), calls=%async_computation | async-start | bytes 1310720 | tf_op jit(solution)/shard_map/all_to_all | solution.py:47
  17.9 247.9 %all-gather.5.cloned.1.call-start = ((), (), s32[]{:S(2)}) async-start(), calls=%async_computation.2 | async-start | bytes 1769472 | tf_op jit(solution)/shard_map/all_gather | solution.py:73
  34.0 4.8 %copy-start.14 = (f32[4,384]{1,0:T(4,128)S(1)}, f32[4,384]{1,0:T(4,128)}, u32[]{:S(2)}) copy-start(f32[4,384]{1,0:T(4,128)} %param.24) | copy-start | bytes 18436
  34.0 4.8 %copy-start.30 = (f32[6]{0:T(128)S(1)}, f32[6]{0:T(128)}, u32[]{:S(2)}) copy-start(f32[6]{0:T(128)} %param.29) | copy-start | bytes 76
  34.0 4.9 %copy-start.31 = (u32[256]{0:T(256)S(1)}, u32[256]{0:T(256)}, u32[]{:S(2)}) copy-start(u32[256]{0:T(256)} %constant.144) | copy-start | bytes 3076
  34.0 6.1 %copy-start.21 = (f32[4,256]{1,0:T(4,128)S(1)}, f32[4,256]{1,0:T(4,128)}, u32[]{:S(2)}) copy-start(f32[4,256]{1,0:T(4,128)} %param.25) | copy-start | bytes 12292
  38.8 53.7 %copy-start.15 = (f32[6]{0:T(128)}, f32[6]{0:T(128)S(1)}, u32[]{:S(2)}) copy-start(f32[6]{0:T(128)S(1)} %neg.22) | copy-start | bytes 76
  40.2 2.7 copy-start.7
  43.8 7.9 %collective-permute-start.2 = (bf16[128,2560]{1,0:T(8,128)(2,1)}, bf16[128,2560]{1,0:T(8,128)(2,1)S(1)}, u32[]{:S(2)}, u32[]{:S(2)}) collective-permute-start(bf16[128,2560]{1,0:T(8,128)(2,1)} %collective-permute-done), channel_id=1, source_target_pairs={{0,1},{1,2},{2,3},{3,4},{4,5},{5,6},{6,7},{7,0},{8,9},{9,10},{10,1... | collective-permute-start | bytes 1966088 | tf_op jit(solution)/shard_map/ppermute | solution.py:27
  43.8 10.3 %collective-permute-start.3 = (bf16[128,2560]{1,0:T(8,128)(2,1)S(1)}, bf16[128,2560]{1,0:T(8,128)(2,1)S(1)}, u32[]{:S(2)}, u32[]{:S(2)}) collective-permute-start(bf16[128,2560]{1,0:T(8,128)(2,1)S(1)} %collective-permute-done.1), channel_id=1, source_target_pairs={{0,7},{1,0},{2,1},{3,2},{4,3},{5,4},{6,5},{7,6},{8,15},{9,8},{10,9... | collective-permute-start | bytes 1966088 | tf_op jit(solution)/shard_map/ppermute | solution.py:32
  51.6 9.9 %collective-permute-start.4 = (bf16[128,2560]{1,0:T(8,128)(2,1)S(1)}, bf16[128,2560]{1,0:T(8,128)(2,1)S(1)}, u32[]{:S(2)}, u32[]{:S(2)}) collective-permute-start(bf16[128,2560]{1,0:T(8,128)(2,1)S(1)} %collective-permute-done.2), channel_id=1, source_target_pairs={{0,1},{1,2},{2,3},{3,4},{4,5},{5,6},{6,7},{7,0},{8,9},{9,10},{10,1... | collective-permute-start | bytes 1966088 | tf_op jit(solution)/shard_map/ppermute | solution.py:27
  54.1 10.8 %collective-permute-start.5 = (bf16[128,2560]{1,0:T(8,128)(2,1)S(1)}, bf16[128,2560]{1,0:T(8,128)(2,1)S(1)}, u32[]{:S(2)}, u32[]{:S(2)}) collective-permute-start(bf16[128,2560]{1,0:T(8,128)(2,1)S(1)} %collective-permute-done.3), channel_id=1, source_target_pairs={{0,7},{1,0},{2,1},{3,2},{4,3},{5,4},{6,5},{7,6},{8,15},{9,8},{10,9... | collective-permute-start | bytes 1966088 | tf_op jit(solution)/shard_map/ppermute | solution.py:32
  61.5 10.0 %collective-permute-start.6 = (bf16[128,2560]{1,0:T(8,128)(2,1)S(1)}, bf16[128,2560]{1,0:T(8,128)(2,1)S(1)}, u32[]{:S(2)}, u32[]{:S(2)}) collective-permute-start(bf16[128,2560]{1,0:T(8,128)(2,1)S(1)} %collective-permute-done.4), channel_id=1, source_target_pairs={{0,1},{1,2},{2,3},{3,4},{4,5},{5,6},{6,7},{7,0},{8,9},{9,10},{10,1... | collective-permute-start | bytes 1966088 | tf_op jit(solution)/shard_map/ppermute | solution.py:27
  72.4 5.1 %copy-start.6 = (bf16[320,8,2,384]{3,1,2,0:T(8,128)(2,1)S(1)}, bf16[320,8,2,384]{3,1,2,0:T(8,128)(2,1)}, u32[]{:S(2)}) copy-start(bf16[320,8,2,384]{3,1,2,0:T(8,128)(2,1)} %copy.123) | copy-start | bytes 11796484
  83.7 5.6 %copy-start.4 = (f32[1024,768]{1,0:T(8,128)}, f32[1024,768]{1,0:T(8,128)S(1)}, u32[]{:S(2)}) copy-start(f32[1024,768]{1,0:T(8,128)S(1)} %convolution_add_fusion) | copy-start | bytes 9437188
  83.7 8.8 %copy-start.13 = (bf16[2560,6]{0,1:T(8,128)(2,1)S(1)}, bf16[2560,6]{0,1:T(8,128)(2,1)}, u32[]{:S(2)}) copy-start(bf16[2560,6]{0,1:T(8,128)(2,1)} %param.21) | copy-start | bytes 92164
  83.7 8.8 %copy-start.23 = (f32[6]{0:T(128)S(1)}, f32[6]{0:T(128)}, u32[]{:S(2)}) copy-start(f32[6]{0:T(128)} %param.28) | copy-start | bytes 76
  83.8 26.6 %collective-permute-start.7 = (f32[3,384]{1,0:T(4,128)S(1)}, f32[3,384]{1,0:T(4,128)S(1)}, u32[]{:S(2)}, u32[]{:S(2)}) collective-permute-start(f32[3,384]{1,0:T(4,128)S(1)} %slice.215), channel_id=1, source_target_pairs={{0,8},{8,16},{16,24},{24,32},{32,40},{40,48},{48,56},{56,64},{64,7... | collective-permute-start | bytes 13832 | tf_op jit(solution)/shard_map/ppermute | solution.py:59
  89.3 17.6 %collective-permute-start.8 = (f32[3,256]{1,0:T(4,128)S(1)}, f32[3,256]{1,0:T(4,128)S(1)}, u32[]{:S(2)}, u32[]{:S(2)}) collective-permute-start(f32[3,256]{1,0:T(4,128)S(1)} %slice.221), channel_id=1, source_target_pairs={{0,8},{8,16},{16,24},{24,32},{32,40},{40,48},{48,56},{56,64},{64,7... | collective-permute-start | bytes 9224 | tf_op jit(solution)/shard_map/ppermute | solution.py:59
  106.9 0.7 copy-start.27
  108.3 1.0 copy-start.2
  109.3 1.8 slice-start
  109.3 1.8 copy-start.22
  122.3 0.6 copy-start.12
  123.0 4.9 %copy-start.8 = (f32[256,6]{0,1:T(8,128)S(1)}, f32[256,6]{0,1:T(8,128)}, u32[]{:S(2)}) copy-start(f32[256,6]{0,1:T(8,128)} %get-tuple-element.235) | copy-start | bytes 18436 | tf_op jit(solution)/shard_map/while
  123.0 4.9 %copy-start.9 = (f32[256,6]{0,1:T(8,128)S(1)}, f32[256,6]{0,1:T(8,128)}, u32[]{:S(2)}) copy-start(f32[256,6]{0,1:T(8,128)} %get-tuple-element.236) | copy-start | bytes 18436 | tf_op jit(solution)/shard_map/while
  145.1 0.6 copy-start.12
  145.7 4.9 %copy-start.8 = (f32[256,6]{0,1:T(8,128)S(1)}, f32[256,6]{0,1:T(8,128)}, u32[]{:S(2)}) copy-start(f32[256,6]{0,1:T(8,128)} %get-tuple-element.235) | copy-start | bytes 18436 | tf_op jit(solution)/shard_map/while
  145.7 4.9 %copy-start.9 = (f32[256,6]{0,1:T(8,128)S(1)}, f32[256,6]{0,1:T(8,128)}, u32[]{:S(2)}) copy-start(f32[256,6]{0,1:T(8,128)} %get-tuple-element.236) | copy-start | bytes 18436 | tf_op jit(solution)/shard_map/while
  167.9 0.6 copy-start.12
  168.5 4.9 %copy-start.8 = (f32[256,6]{0,1:T(8,128)S(1)}, f32[256,6]{0,1:T(8,128)}, u32[]{:S(2)}) copy-start(f32[256,6]{0,1:T(8,128)} %get-tuple-element.235) | copy-start | bytes 18436 | tf_op jit(solution)/shard_map/while
  168.5 4.9 %copy-start.9 = (f32[256,6]{0,1:T(8,128)S(1)}, f32[256,6]{0,1:T(8,128)}, u32[]{:S(2)}) copy-start(f32[256,6]{0,1:T(8,128)} %get-tuple-element.236) | copy-start | bytes 18436 | tf_op jit(solution)/shard_map/while
  190.7 0.6 copy-start.12
  191.3 4.9 %copy-start.8 = (f32[256,6]{0,1:T(8,128)S(1)}, f32[256,6]{0,1:T(8,128)}, u32[]{:S(2)}) copy-start(f32[256,6]{0,1:T(8,128)} %get-tuple-element.235) | copy-start | bytes 18436 | tf_op jit(solution)/shard_map/while
  191.3 4.9 %copy-start.9 = (f32[256,6]{0,1:T(8,128)S(1)}, f32[256,6]{0,1:T(8,128)}, u32[]{:S(2)}) copy-start(f32[256,6]{0,1:T(8,128)} %get-tuple-element.236) | copy-start | bytes 18436 | tf_op jit(solution)/shard_map/while
  208.1 13.0 %copy-start.11 = (f32[1024,6]{0,1:T(8,128)S(1)}, f32[1024,6]{0,1:T(8,128)}, u32[]{:S(2)}) copy-start(f32[1024,6]{0,1:T(8,128)} %get-tuple-element.181) | copy-start | bytes 73732
  208.1 13.0 %copy-start.16 = (f32[6]{0:T(128)S(1)}, f32[6]{0:T(128)}, u32[]{:S(2)}) copy-start(f32[6]{0:T(128)} %copy-done.15) | copy-start | bytes 76
  208.1 15.2 %copy-start.24 = (f32[1,1,6]{2,1,0:T(1,128)S(1)}, f32[1,1,6]{2,1,0:T(1,128)}, u32[]{:S(2)}) copy-start(f32[1,1,6]{2,1,0:T(1,128)} %get-tuple-element.177) | copy-start | bytes 76
  218.6 0.9 copy-start.1
  237.3 28.6 %copy-start.17 = (f32[6]{0:T(128)S(1)}, f32[6]{0:T(128)}, u32[]{:S(2)}) copy-start(f32[6]{0:T(128)} %get-tuple-element.176) | copy-start | bytes 76
  237.3 28.6 %copy-start.18 = (f32[6]{0:T(128)S(1)}, f32[6]{0:T(128)}, u32[]{:S(2)}) copy-start(f32[6]{0:T(128)} %get-tuple-element.178) | copy-start | bytes 76
  237.3 28.6 %copy-start.19 = (f32[6]{0:T(128)S(1)}, f32[6]{0:T(128)}, u32[]{:S(2)}) copy-start(f32[6]{0:T(128)} %get-tuple-element.179) | copy-start | bytes 76
  237.3 28.5 %copy-start.20 = (f32[6]{0:T(128)S(1)}, f32[6]{0:T(128)}, u32[]{:S(2)}) copy-start(f32[6]{0:T(128)} %get-tuple-element.180) | copy-start | bytes 76
  237.3 28.5 %copy-start.26 = (f32[6]{0:T(128)S(1)}, f32[6]{0:T(128)}, u32[]{:S(2)}) copy-start(f32[6]{0:T(128)} %get-tuple-element.175) | copy-start | bytes 76
  265.8 2.2 copy-start.3
  268.0 1.4 copy-start.5
  268.0 1.4 copy-start.28
  273.1 16.4 %copy-start.25 = (f32[384]{0:T(512)S(1)}, f32[384]{0:T(512)}, u32[]{:S(2)}) copy-start(f32[384]{0:T(512)} %param.31) | copy-start | bytes 4612
Sparse Core Ops, SparseCore 0:
  221.1 44.6 all-gather.4
